TPU v7x, 32 devices: a whole 2x2x4 slice. The times are simulated.
32 devices in a mesh: vocab: 8 (over z, y), layer: 4 (over x, core).
Axes of the slice: x: 2, y: 2, z: 4, core: 2. Of those that a mesh axis runs over, the one named last changes fastest.
Arguments:
- residual: bfloat16 [1024, 8192], P('layer', 'vocab'), may hold values from -40 to 40
- gain: bfloat16 [1, 8192], P(None, 'vocab'), may hold values from 0.25 to 1.75
- unembed: bfloat16 [8192, 128256], P(None, ('vocab', 'layer')), may hold values from -0.22097087 to 0.22097087
Outputs:
- log_probs: float32 [1024, 128256], P('layer', 'vocab')
All inputs are finite; a program needn't handle non-finite values.
Results may differ from a plain program's by a relative error of at most 0.0003.
Values may be sent and summed in bfloat16 or wider, within the bound.
No kernel may reach another device: no remote copies, remote signals or barrier semaphores. Data moves between devices by JAX's collectives and lax.ppermute only.
A program may use at most 192 MiB of HBM per device.

v0:
```python
import jax
import jax.numpy as jnp
from jax import lax
from jax.sharding import PartitionSpec as P

D = 8192


def joined(shard, axis, combine):
    everything = jax.tree.map(lambda part: lax.all_gather(part, axis), shard)
    initial = jax.tree.map(lambda part: part[0], everything)

    def lap(k, so_far):
        return combine(so_far, jax.tree.map(lambda part: part[k], everything))

    return lax.fori_loop(1, lax.axis_size(axis), lap, initial)


def combine_pairs(earlier, later):
    highest = jnp.maximum(earlier[0], later[0])
    totals = earlier[1] * jnp.exp(earlier[0] - highest) + later[1] * jnp.exp(later[0] - highest)
    return (highest, totals)


def local(residual, gain, unembed):
    full_rows, full_gain = (
        lax.all_gather(residual, "vocab", axis=1, tiled=True),
        lax.all_gather(gain, "vocab", axis=1, tiled=True),
    )
    all_rows = lax.all_gather(full_rows, "layer", axis=0, tiled=True)
    widened = all_rows.astype(jnp.float32)
    squares = jnp.sum(widened * widened, axis=1)
    scaled = (widened * full_gain.astype(jnp.float32)).astype(jnp.bfloat16)
    products = jnp.dot(scaled, unembed, preferred_element_type=jnp.float32)
    inverse = lax.rsqrt(squares / D + 1e-05)
    logits = products * inverse[:, None]
    local_max = jnp.max(logits, axis=1)
    local_sums = jnp.sum(jnp.exp(logits - local_max[:, None]), axis=1)
    highest, totals = joined((local_max, local_sums), ("vocab", "layer"), combine_pairs)
    lse = highest + jnp.log(totals)
    log_values = logits - lse[:, None]
    return lax.all_to_all(log_values, "layer", split_axis=0, concat_axis=1, tiled=True)


def solution(mesh):
    placed = (P("layer", "vocab"), P(None, "vocab"), P(None, ("vocab", "layer")))
    return jax.shard_map(
        local, mesh=mesh, in_specs=placed, out_specs=P("layer", "vocab"), check_vma=False
    )
```

profile of v0, /device:TPU:0, one launch (start us, length us, event | category | flops | bytes accessed | tf_op | source)
XLA Modules:
  0.0 570.1 jit_solution(13721698906693469134)
XLA Ops:
  6.5 0.0 all-gather.5.cloned.1.call-start
  6.5 0.7 all-gather.5.cloned.1.call-update
  7.3 0.0 all-gather.7.cloned.1.call-start
  7.3 77.7 %all-gather.5.cloned.1.call-done = bf16[256,8192]{1,0:T(8,128)(2,1)} async-done(((bf16[256,1024]{1,0:T(8,128)(2,1)}), bf16[256,8192]{1,0:T(8,128)(2,1)}) %all-gather.5.cloned.1.call-update) | async-done | bytes 4194320 | tf_op jit(solution)/shard_map/all_gather | solution.py:27
  85.0 0.0 all-gather.7.cloned.1.call-update
  85.1 30.7 %all_gather.23 = bf16[1,8192]{1,0:T(2,128)(2,1)S(1)} all-gather(bf16[1,1024]{1,0:T(2,128)(2,1)} %param.6), channel_id=1, replica_groups=mesh['vocab'=8,'layer'=4] {'vocab'}, dimensions={1}, use_global_device_ids=true | all-gather | bytes 18432 | tf_op jit(solution)/shard_map/all_gather | solution.py:28
  115.9 75.2 %all-gather.7.cloned.1.call-done = bf16[1024,8192]{1,0:T(8,128)(2,1)} async-done(((bf16[256,8192]{1,0:T(8,128)(2,1)}), bf16[1024,8192]{1,0:T(8,128)(2,1)}) %all-gather.7.cloned.1.call-update) | async-done | bytes 16777232 | tf_op jit(solution)/shard_map/all_gather | solution.py:30
  191.1 7.2 %fusion.1 = f32[1024]{0:T(1024)S(1)} fusion(bf16[1024,8192]{1,0:T(8,128)(2,1)} %all-gather.7.cloned.1.call-done), kind=kLoop, calls=%fused_computation.6 | loop fusion | flops 25164800 | bytes 16781312 | tf_op jit(solution)/shard_map/reduce_sum | solution.py:32
  198.3 79.6 %multiply_reduce_fusion = (f32[1024]{0:T(1024)S(1)}, f32[1024,4008]{0,1:T(8,128)}) fusion(f32[1024]{0:T(1024)S(1)} %add_rsqrt_fusion, bf16[8192,4008]{0,1:T(8,128)(2,1)} %param.7, bf16[1024,8192]{1,0:T(8,128)(2,1)} %all-gather.7.cloned.1.call-done, f32[8192]{0:T(1024)S(1)} %bitcast.21), kind=kOutput, calls=%fused_computation.12 | convolution fusion | flops 67276455936 | bytes 98902016 | tf_op jit(solution)/shard_map/dot_general | solution.py:34
  277.9 8.4 %exponential_reduce_fusion = f32[1024]{0:T(1024)S(1)} fusion(f32[1024,4008]{0,1:T(8,128)} %get-tuple-element.155, f32[1024]{0:T(1024)S(1)} %get-tuple-element.154, f32[1024]{0:T(1024)S(1)} %add_rsqrt_fusion), kind=kLoop, calls=%fused_computation.10 | loop fusion | flops 12311552 | bytes 16429056 | tf_op jit(solution)/shard_map/reduce_sum | solution.py:38
  286.3 40.9 %all-gather.1 = f32[32768]{0:T(1024)S(1)} all-gather(f32[1024]{0:T(1024)S(1)} %exponential_reduce_fusion), channel_id=3, replica_groups=mesh['vocab'=8,'layer'=4] {'vocab','layer'}, dimensions={0}, use_global_device_ids=true | all-gather | bytes 135168 | tf_op jit(solution)/shard_map/all_gather | solution.py:10
  327.2 37.0 %all-gather = f32[32768]{0:T(1024)S(1)} all-gather(f32[1024]{0:T(1024)S(1)} %get-tuple-element.154), channel_id=2, replica_groups=mesh['vocab'=8,'layer'=4] {'vocab','layer'}, dimensions={0}, use_global_device_ids=true | all-gather | bytes 135168 | tf_op jit(solution)/shard_map/all_gather | solution.py:10
  364.2 1.8 while.17
  366.1 7.2 %multiply_subtract_fusion = f32[1024,4008]{0,1:T(8,128)S(1)} fusion(f32[1024,4008]{0,1:T(8,128)} %get-tuple-element.155, f32[1024]{0:T(1024)S(1)} %log_add_fusion, f32[1024]{0:T(1024)S(1)} %add_rsqrt_fusion), kind=kLoop, calls=%fused_computation.11 | loop fusion | flops 8208384 | bytes 32841728 | tf_op jit(solution)/shard_map/sub | solution.py:41
  373.3 1.8 copy.8
  375.1 182.2 %all_to_all.19 = f32[4,256,4008]{1,2,0:T(8,128)S(1)} all-to-all(f32[4,256,4008]{1,2,0:T(8,128)S(1)} %bitcast.17), channel_id=1, replica_groups=mesh['vocab'=8,'layer'=4] {'layer'}, dimensions={0} | all-to-all | bytes 32833536 | tf_op jit(solution)/shard_map/all_to_all | solution.py:42
  557.3 6.0 %copy.19 = f32[256,16032]{0,1:T(8,128)} copy(f32[256,16032]{0,1:T(8,128)S(1)} %bitcast.18) | data formatting | bytes 32833536
  (69 shorter events, 0.9 us)
Async XLA Ops:
  6.5 78.5 %all-gather.5.cloned.1.call-start = ((), (), s32[]{:S(2)}) async-start(), calls=%async_computation.1 | async-start | bytes 4718592 | tf_op jit(solution)/shard_map/all_gather | solution.py:27
  7.3 183.8 %all-gather.7.cloned.1.call-start = ((), (), s32[]{:S(2)}) async-start(), calls=%async_computation.2 | async-start | bytes 20971520 | tf_op jit(solution)/shard_map/all_gather | solution.py:30
Sparse Core Ops, SparseCore 0:
  9.5 75.4 all-gather.4
  86.6 104.4 all-gather.6
where the time goes:
time: 570 us
  blocking collectives  291 us (51%)
  waiting for transfers between devices  154 us (27%)
  matrix products  79.6 us (14%)
  other arithmetic  23.2 us (4%)
  between operations  13.5 us (2%)
  local copies, waits for them, and re-layouts  8.36 us (1%)
    all_to_all x1, blocking collectives, local(): lax.all_to_all(log_values, 'layer', split_axis=0, concat_axis=1, tiled=True)  182 us
    dot_general x1, matrix products, local(): products = jnp.dot(scaled, unembed, preferred_element_type=jnp.float32)  79.6 us
    all_gather x2, blocking collectives, joined(): everything = jax.tree.map(lambda part: lax.all_gather(part, axis), shard)  77.9 us
    all_gather x1, waiting for transfers between devices, local(): lax.all_gather(residual, 'vocab', axis=1, tiled=True)  77.7 us
    all_gather x1, waiting for transfers between devices, local(): all_rows = lax.all_gather(full_rows, 'layer', axis=0, tiled=True)  75.2 us
    all_gather x1, blocking collectives, local(): lax.all_gather(gain, 'vocab', axis=1, tiled=True)  30.7 us
  transfers between devices with their start and end apart: 2, of which 2 were waited for; matrix products, arithmetic and copies ran while one was open for 0% of the time, Pallas kernels for 0%

commit v1 on v0

--- a/solution.py
+++ b/solution.py
@@ -24,7 +24,7 @@
 
 def local(residual, gain, unembed):
     full_rows, full_gain = (
-        lax.all_gather(residual, "vocab", axis=1, tiled=True),
+        jnp.concatenate(lax.all_gather(residual, "vocab"), axis=1),
         lax.all_gather(gain, "vocab", axis=1, tiled=True),
     )
     all_rows = lax.all_gather(full_rows, "layer", axis=0, tiled=True)

time: 570 us -> 582 us (1.021)
  local copies, waits for them, and re-layouts: 8.36 us -> 14.8 us
    reshape x0 -> x1, local copies, waits for them, and re-layouts: none -> 6.42 us  [local(): jnp.concatenate(lax.all_gather(residual, 'vocab'), axis=1)]
where the time goes in v1:
time: 582 us; the launch traced here: 581 us
  blocking collectives  291 us (50%)
  waiting for transfers between devices  154 us (26%)
  matrix products  80.6 us (14%)
  other arithmetic  26.3 us (5%)
  local copies, waits for them, and re-layouts  14.8 us (3%)
  between operations  13.5 us (2%)
    all_to_all x1, blocking collectives, local(): lax.all_to_all(log_values, 'layer', split_axis=0, concat_axis=1, tiled=True)  182 us
    dot_general x1, matrix products, local(): products = jnp.dot(scaled, unembed, preferred_element_type=jnp.float32)  80.6 us
    all_gather x2, blocking collectives, joined(): everything = jax.tree.map(lambda part: lax.all_gather(part, axis), shard)  77.9 us
    all_gather x1, waiting for transfers between devices, local(): lax.all_gather(residual, 'vocab')  77.7 us
    all_gather x1, waiting for transfers between devices, local(): all_rows = lax.all_gather(full_rows, 'layer', axis=0, tiled=True)  76 us
    all_gather x1, blocking collectives, local(): lax.all_gather(gain, 'vocab', axis=1, tiled=True)  30.7 us
  transfers between devices with their start and end apart: 2, of which 2 were waited for; matrix products, arithmetic and copies ran while one was open for 0% of the time, Pallas kernels for 0%

profile of v1, /device:TPU:0, one launch (start us, length us, event | category | flops | bytes accessed | tf_op | source)
XLA Modules:
  0.0 581.5 jit_solution(4150895280909002197)
XLA Ops:
  6.5 0.0 all-gather.8.cloned.1.call-start
  6.5 0.7 all-gather.8.cloned.1.call-update
  7.3 0.0 all-gather.6.cloned.1.call-start
  7.3 77.7 %all-gather.8.cloned.1.call-done = bf16[2048,1024]{1,0:T(8,128)(2,1)} async-done(((bf16[256,1024]{1,0:T(8,128)(2,1)}), bf16[2048,1024]{1,0:T(8,128)(2,1)}) %all-gather.8.cloned.1.call-update) | async-done | bytes 4194320 | tf_op jit(solution)/shard_map/all_gather | solution.py:27
  85.0 6.4 %copy.8 = bf16[256,8,1024]{0,2,1:T(8,128)(2,1)} copy(bf16[256,8,1024]{2,0,1:T(8,128)(2,1)} %bitcast.24) | data formatting | bytes 8388608 | tf_op jit(solution)/shard_map/reshape | solution.py:27
  91.4 0.0 all-gather.6.cloned.1.call-update
  91.5 30.7 %all_gather.27 = bf16[1,8192]{1,0:T(2,128)(2,1)S(1)} all-gather(bf16[1,1024]{1,0:T(2,128)(2,1)} %param.6), channel_id=1, replica_groups=mesh['vocab'=8,'layer'=4] {'vocab'}, dimensions={1}, use_global_device_ids=true | all-gather | bytes 18432 | tf_op jit(solution)/shard_map/all_gather | solution.py:28
  122.2 76.0 %all-gather.6.cloned.1.call-done = bf16[1024,8192]{0,1:T(8,128)(2,1)} async-done(((bf16[256,8192]{0,1:T(8,128)(2,1)}), bf16[1024,8192]{0,1:T(8,128)(2,1)}) %all-gather.6.cloned.1.call-update) | async-done | bytes 16777232 | tf_op jit(solution)/shard_map/all_gather | solution.py:30
  198.3 10.3 %fusion.1 = f32[1024]{0:T(1024)S(1)} fusion(bf16[1024,8192]{0,1:T(8,128)(2,1)} %all-gather.6.cloned.1.call-done), kind=kLoop, calls=%fused_computation.6 | loop fusion | flops 25164800 | bytes 16781312 | tf_op jit(solution)/shard_map/reduce_sum | solution.py:32
  208.6 80.6 %multiply_reduce_fusion = (f32[1024]{0:T(1024)S(1)}, f32[1024,4008]{0,1:T(8,128)}) fusion(f32[1024]{0:T(1024)S(1)} %add_rsqrt_fusion, bf16[8192,4008]{0,1:T(8,128)(2,1)} %param.7, bf16[1024,8192]{0,1:T(8,128)(2,1)} %all-gather.6.cloned.1.call-done, f32[8192]{0:T(1024)S(1)} %bitcast.27), kind=kOutput, calls=%fused_computation.12 | convolution fusion | flops 67276455936 | bytes 98902016 | tf_op jit(solution)/shard_map/dot_general | solution.py:34
  289.2 8.4 %exponential_reduce_fusion = f32[1024]{0:T(1024)S(1)} fusion(f32[1024,4008]{0,1:T(8,128)} %get-tuple-element.155, f32[1024]{0:T(1024)S(1)} %get-tuple-element.154, f32[1024]{0:T(1024)S(1)} %add_rsqrt_fusion), kind=kLoop, calls=%fused_computation.10 | loop fusion | flops 12311552 | bytes 16429056 | tf_op jit(solution)/shard_map/reduce_sum | solution.py:38
  297.6 40.9 %all-gather.2 = f32[32768]{0:T(1024)S(1)} all-gather(f32[1024]{0:T(1024)S(1)} %exponential_reduce_fusion), channel_id=4, replica_groups=mesh['vocab'=8,'layer'=4] {'vocab','layer'}, dimensions={0}, use_global_device_ids=true | all-gather | bytes 135168 | tf_op jit(solution)/shard_map/all_gather | solution.py:10
  338.5 37.0 %all-gather.1 = f32[32768]{0:T(1024)S(1)} all-gather(f32[1024]{0:T(1024)S(1)} %get-tuple-element.154), channel_id=3, replica_groups=mesh['vocab'=8,'layer'=4] {'vocab','layer'}, dimensions={0}, use_global_device_ids=true | all-gather | bytes 135168 | tf_op jit(solution)/shard_map/all_gather | solution.py:10
  375.6 1.8 while.17
  377.4 7.2 %multiply_subtract_fusion = f32[1024,4008]{0,1:T(8,128)S(1)} fusion(f32[1024,4008]{0,1:T(8,128)} %get-tuple-element.155, f32[1024]{0:T(1024)S(1)} %log_add_fusion, f32[1024]{0:T(1024)S(1)} %add_rsqrt_fusion), kind=kLoop, calls=%fused_computation.11 | loop fusion | flops 8208384 | bytes 32841728 | tf_op jit(solution)/shard_map/sub | solution.py:41
  384.6 1.8 copy.12
  386.4 182.2 %all_to_all.19 = f32[4,256,4008]{1,2,0:T(8,128)S(1)} all-to-all(f32[4,256,4008]{1,2,0:T(8,128)S(1)} %bitcast.21), channel_id=1, replica_groups=mesh['vocab'=8,'layer'=4] {'layer'}, dimensions={0} | all-to-all | bytes 32833536 | tf_op jit(solution)/shard_map/all_to_all | solution.py:42
  568.6 6.0 %copy.23 = f32[256,16032]{0,1:T(8,128)} copy(f32[256,16032]{0,1:T(8,128)S(1)} %bitcast.22) | data formatting | bytes 32833536
  (69 shorter events, 0.9 us)
Async XLA Ops:
  6.5 78.5 %all-gather.8.cloned.1.call-start = ((), (), s32[]{:S(2)}) async-start(), calls=%async_computation.2 | async-start | bytes 4718592 | tf_op jit(solution)/shard_map/all_gather | solution.py:27
  7.3 191.0 %all-gather.6.cloned.1.call-start = ((), (), s32[]{:S(2)}) async-start(), calls=%async_computation.1 | async-start | bytes 20971520 | tf_op jit(solution)/shard_map/all_gather | solution.py:30
Sparse Core Ops, SparseCore 0:
  9.5 75.5 all-gather.7
  91.6 106.6 all-gather.5
